TPU v7x, 512 devices: a whole 4x8x8 slice. The times are simulated.
512 devices in a mesh: gy: 64 (over z, y_lo, core), gz: 8 (over y_hi, x).
Axes of the slice: x: 4, y: 8 (y_hi: 2, y_lo: 4; y = y_hi * 4 + y_lo), z: 8, core: 2. Of those that a mesh axis runs over, the one named last changes fastest.
Arguments:
- omega: float32 [3, 1024, 512, 128], P(None, 'gy', 'gz'), may hold values from -6 to 6
- velocity: float32 [3, 1024, 512, 128], P(None, 'gy', 'gz'), may hold values from -6 to 6
- point_owner: int32 [1152], replicated, may hold values from 2 to 477, as said below
- point_cells: int32 [3, 1152], replicated, may hold values from 1 to 125, as said below
- point_frac: float32 [3, 1152], replicated, may hold values from 0 to 1
- chord: float32 [1152], replicated, may hold values from 0.2 to 1
- twist: float32 [1152], replicated, may hold values from -0.3 to 0.3
- angle_step: int32 [1], replicated, may hold values from 0 to 719
Outputs:
- omega_out: float32 [3, 1024, 512, 128], P(None, 'gy', 'gz')
- blade_sources: float32 [3, 1152], replicated
Inputs may be any that keep to these rules, and one draw needn't show every extreme that they name: `point_owner`: turbine t's points lie in spanwise blocks t * 10 to (t + 1) * 10 - 1 and in the 4 vertical blocks from (4) // 2 on; no block holds more than 9 points, and in every turbine one block holds exactly 9. `point_cells`: streamwise cells lie in 1 to 125, spanwise in 1 to 13, vertical in 1 to 61; all points of a turbine share one streamwise cell.
All inputs are finite; a program needn't handle non-finite values.
Results may differ from a plain program's by a relative error of at most 0.0003.
Values sent between devices are 32-bit elements; how exact they have to be, the bound alone decides.
A program may use at most 128 MiB of HBM per device.

v0:
```python
import jax
import jax.numpy as jnp
from jax import lax
from jax.sharding import Mesh
from jax.sharding import PartitionSpec as P

TURBINES = 6
BLADES = 3
BP = 64
GY = ("gy_0", "gy_1", "gy_2")
GZ = ("gz_0", "gz_1")
GY_GZ = ("gy_0", "gy_1", "gy_2", "gz_0", "gz_1")
section_step = 0.4
viscosity = 0.05
tip_speed = 3.0
turn_step = 2.0 * 3.141592653589793 / 720.0


def by_axis(x, axes):
    for axis in axes:
        x = lax.psum(x, axis)
    return x


def with_halo(x, sides, width):
    edges = {}
    for axis, dim in sides:
        size, length = (lax.axis_size(axis), x.shape[dim])
        up = [(i, (i + 1) % size) for i in range(size - 1)]
        last = lax.slice_in_dim(x, length - width, length, axis=dim)
        initial = lax.slice_in_dim(x, 0, width, axis=dim)
        edges[dim] = (
            lax.ppermute(last, axis, up),
            lax.ppermute(initial, axis, [(b, a) for a, b in up]),
        )
    done = []
    for _, dim in sides:
        low, high = edges[dim]
        around = [(width, width) if d in done else (0, 0) for d in range(x.ndim)]
        x = jnp.concatenate([jnp.pad(low, around), x, jnp.pad(high, around)], axis=dim)
        done.append(dim)
    return x


def with_halo_2(x, sides, width):
    for axis, dim in sides:
        size, length = (lax.axis_size(axis), x.shape[dim])
        up = [(i, (i + 1) % size) for i in range(size - 1)]
        down = [(j, i) for i, j in up]
        last = lax.slice_in_dim(x, length - width, length, axis=dim)
        initial = lax.slice_in_dim(x, 0, width, axis=dim)
        before = lax.ppermute(last, axis, up)
        after = lax.ppermute(initial, axis, down)
        x = jnp.concatenate([before, x, after], axis=dim)
    return x


def remesh_kernel(shift):
    mag = jnp.abs(shift)
    inner = 1.0 - 2.5 * mag * mag + 1.5 * mag * mag * mag
    outer = 0.5 * (2.0 - mag) * (2.0 - mag) * (1.0 - mag)
    return jnp.where(mag < 1.0, inner, jnp.where(mag < 2.0, outer, 0.0))


def shifted(padded, axis, offset):
    index = []
    for dim in range(4):
        if dim == 0:
            index.append(slice(None))
        elif dim == axis:
            index.append(slice(offset, offset + padded.shape[dim] - 4))
        else:
            index.append(slice(2, padded.shape[dim] - 2))
    return padded[tuple(index)]


def centered_first(padded, axis):
    return (
        shifted(padded, axis, 0)
        - 8.0 * shifted(padded, axis, 1)
        + 8.0 * shifted(padded, axis, 3)
        - shifted(padded, axis, 4)
    ) / 12.0


def centered_second(padded, axis):
    return (
        -shifted(padded, axis, 0)
        + 16.0 * shifted(padded, axis, 1)
        - 30.0 * shifted(padded, axis, 2)
        + 16.0 * shifted(padded, axis, 3)
        - shifted(padded, axis, 4)
    ) / 12.0


def remesh_padded(field, displace, axis):
    length = field.shape[axis] - 4
    total = jnp.zeros(field.shape[:axis] + (length,) + field.shape[axis + 1 :], jnp.float32)
    for offset in range(-2, 3):
        start = 2 - offset
        part = lax.slice_in_dim(field, start, start + length, axis=axis)
        moved = lax.slice_in_dim(displace, start, start + length, axis=axis - 1)
        total = total + remesh_kernel(offset - moved)[None] * part
    return total


def blade_forces(point_velocity, chord, twist, angle_step):
    count = point_velocity.shape[1]
    points = jnp.arange(count, dtype=jnp.int32)
    station = points % BP
    blade = points // BP % BLADES
    theta = angle_step[0].astype(
        jnp.float32
    ) * turn_step + 2.0 * 3.141592653589793 / 3.0 * blade.astype(jnp.float32)
    radius = (station.astype(jnp.float32) + 0.5) / BP
    cos_t = jnp.cos(theta)
    sin_t = jnp.sin(theta)
    rel_x = point_velocity[0]
    rel_y = point_velocity[1] + tip_speed * radius * sin_t
    rel_z = point_velocity[2] - tip_speed * radius * cos_t
    rel_t = -sin_t * rel_y + cos_t * rel_z
    speed = jnp.sqrt(rel_x * rel_x + rel_t * rel_t + 1.0)
    gamma = 3.141592653589793 * chord * (rel_x * jnp.cos(twist) + rel_t * jnp.sin(twist))
    blades = gamma.reshape(-1, BP)
    before = jnp.concatenate([jnp.zeros((blades.shape[0], 1), jnp.float32), blades[:, :-1]], axis=1)
    shed = (blades - before).reshape(-1)
    return jnp.stack(
        [
            shed * rel_x / speed,
            gamma * cos_t + shed * rel_y / speed,
            gamma * sin_t + shed * rel_z / speed,
        ]
    )


def point_tables(
    cells,
    fracs,
    owner_span,
    owner_vert,
    span_index,
    vert_index,
    span_cells,
    vert_cells,
    axial_cells,
):
    rows_x = jnp.arange(axial_cells, dtype=jnp.int32)
    rows_y = jnp.arange(span_cells, dtype=jnp.int32)
    rows_z = jnp.arange(vert_cells, dtype=jnp.int32)
    gap_x = rows_x[:, None] - cells[0][None, :]
    gap_y = (
        span_index * span_cells
        + rows_y[:, None]
        - owner_span[None, :] * span_cells
        - cells[1][None, :]
    )
    gap_z = (
        vert_index * vert_cells
        + rows_z[:, None]
        - owner_vert[None, :] * vert_cells
        - cells[2][None, :]
    )
    table_x = remesh_kernel(gap_x.astype(jnp.float32) - fracs[0][None, :])
    table_y = remesh_kernel(gap_y.astype(jnp.float32) - fracs[1][None, :])
    table_z = remesh_kernel(gap_z.astype(jnp.float32) - fracs[2][None, :])
    return (table_x, table_y, table_z)


def on_device(omega, velocity, point_owner, point_cells, point_frac, chord, twist, angle_step):
    span_cells, vert_cells, axial_cells = (omega.shape[1], omega.shape[2], omega.shape[3])
    span_count = lax.axis_size(GY)
    vert_count = lax.axis_size(GZ)
    span_index = lax.axis_index(GY)
    vert_index = lax.axis_index(GZ)
    owner_span = point_owner // vert_count
    owner_vert = point_owner % vert_count
    highest = lax.Precision.HIGHEST
    busiest = 2 * (BLADES * BP) // (span_count // TURBINES * max(vert_count // 2, 1))
    my_block = span_index * vert_count + vert_index
    points = jnp.arange(point_owner.shape[0], dtype=jnp.int32)
    ranking = jnp.where(point_owner == my_block, points, points + point_owner.shape[0])
    picked = jnp.argsort(ranking, stable=True)[:busiest]
    selector = (picked[:, None] == points[None, :]).astype(jnp.float32)
    table_x, table_y, table_z = point_tables(
        point_cells[:, picked],
        point_frac[:, picked],
        owner_span[picked],
        owner_vert[picked],
        span_index,
        vert_index,
        span_cells,
        vert_cells,
        axial_cells,
    )
    columns = jnp.dot(
        velocity.reshape(-1, axial_cells),
        table_x,
        precision=highest,
        preferred_element_type=jnp.float32,
    )
    columns = columns.reshape(3, span_cells, vert_cells, -1)
    compact = jnp.einsum("cyzq,yq,zq->cq", columns, table_y, table_z, precision=highest)
    partial_velocity = jnp.dot(
        compact, selector, precision=highest, preferred_element_type=jnp.float32
    )
    point_velocity = by_axis(partial_velocity, GY_GZ)
    sources = blade_forces(point_velocity, chord, twist, angle_step)
    local_sources = sources[:, picked]
    spread = jnp.einsum("cq,yq,zq->cyzq", local_sources, table_y, table_z, precision=highest)
    smear = jnp.dot(
        spread.reshape(-1, spread.shape[3]),
        table_x.T,
        precision=highest,
        preferred_element_type=jnp.float32,
    )
    smear = smear.reshape(3, span_cells, vert_cells, axial_cells)
    omega_rim, velocity_rim = (
        with_halo(omega, ((GY, 1), (GZ, 2)), 2),
        with_halo(velocity, ((GY, 1), (GZ, 2)), 2),
    )
    axial_pads = ((0, 0), (0, 0), (0, 0), (2, 2))
    omega_pad = jnp.pad(omega_rim, axial_pads)
    velocity_pad = jnp.pad(velocity_rim, axial_pads)
    stretch = jnp.zeros_like(omega)
    laplace = jnp.zeros_like(omega)
    for axis in range(3):
        stretch = stretch + omega[2 - axis][None] * centered_first(velocity_pad, 3 - axis)
        laplace = laplace + centered_second(omega_pad, axis + 1)
    section = omega + section_step * (stretch + viscosity * laplace + smear)
    shift_x = jnp.clip(section_step * velocity[0], -1.0, 1.0)
    moved_x = remesh_padded(
        jnp.pad(section, axial_pads), jnp.pad(shift_x, ((0, 0), (0, 0), (2, 2))), 3
    )
    shift_z = jnp.clip(section_step * velocity_rim[2][2 : span_cells + 2, :, :], -1.0, 1.0)
    span_rim = with_halo_2(moved_x, ((GY, 1),), 2)
    shift_y = jnp.clip(section_step * velocity_rim[1][:, 2 : vert_cells + 2, :], -1.0, 1.0)
    moved_mid = remesh_padded(span_rim, shift_y, 1)
    moved_y = with_halo_2(moved_mid, ((GZ, 2),), 2)
    omega_out = remesh_padded(moved_y, shift_z, 2)
    return (omega_out, sources)


def solution(mesh):
    split = Mesh(mesh.devices.reshape(8, 4, 2, 2, 4), ("gy_0", "gy_1", "gy_2", "gz_0", "gz_1"))
    placed = (P(None, GY, GZ, None), P(None, GY, GZ, None), P(), P(), P(), P(), P(), P())
    return jax.shard_map(
        on_device,
        mesh=split,
        in_specs=placed,
        out_specs=(P(None, GY, GZ, None), P()),
        check_vma=False,
    )
```

profile of v0, /device:TPU:96, one launch (start us, length us, event | category | flops | bytes accessed | tf_op | source)
XLA Modules:
  0.0 213.7 jit_solution(1090650749825777599)
XLA Ops:
  0.7 1.9 fusion.256
  2.6 1.9 collective-permute-start.1
  4.5 1.8 fusion.258
  6.3 2.7 %collective-permute-start.4 = (f32[3,2,64,128]{3,2,1,0:T(8,128)}, f32[3,2,64,128]{3,2,1,0:T(8,128)}, u32[]{:S(2)}, u32[]{:S(2)}) collective-permute-start(f32[3,2,64,128]{3,2,1,0:T(8,128)} %get-tuple-element.35), channel_id=1, source_target_pairs={{0,8},{8,16},{16,24},{24,32},{32,40},{40,48},{48,56},{56,64},{64,7... | collective-permute-start | bytes 589832 | tf_op jit(solution)/shard_map/ppermute | solution.py:33
  9.0 0.7 fusion.255
  9.7 3.4 %collective-permute-start = (f32[3,16,2,128]{3,2,1,0:T(2,128)}, f32[3,16,2,128]{3,2,1,0:T(2,128)}, u32[]{:S(2)}, u32[]{:S(2)}) collective-permute-start(f32[3,16,2,128]{3,2,1,0:T(2,128)} %get-tuple-element.28), channel_id=1, source_target_pairs={{0,1},{1,2},{2,3},{3,4},{4,5},{5,6},{6,7},{8,9},{9,10},{10,11},{11... | collective-permute-start | bytes 147464 | tf_op jit(solution)/shard_map/ppermute | solution.py:33
  13.1 8.5 %collective-permute-start.3 = (f32[3,16,2,128]{3,2,1,0:T(2,128)}, f32[3,16,2,128]{3,2,1,0:T(2,128)S(1)}, u32[]{:S(2)}, u32[]{:S(2)}) collective-permute-start(f32[3,16,2,128]{3,2,1,0:T(2,128)} %get-tuple-element.29), channel_id=1, source_target_pairs={{1,0},{2,1},{3,2},{4,3},{5,4},{6,5},{7,6},{9,8},{10,9},{11,10},{12... | collective-permute-start | bytes 147464 | tf_op jit(solution)/shard_map/ppermute | solution.py:34
  21.6 1.7 fusion.257
  23.3 1.9 collective-permute-start.6
  25.3 5.0 %sort.17 = (s32[1152]{0:T(1024)}, s32[1152]{0:T(1024)S(1)}) sort(s32[1152]{0:T(1024)S(1)} %get-tuple-element.61, s32[1152]{0:T(1024)S(1)} %iota.43), dimensions={0}, to_apply=%region_0.1 | sort | flops 12672 | bytes 18432 | tf_op jit(solution)/shard_map/jit(argsort)/sort | solution.py:182
  33.6 2.1 convolution_bitcast_fusion
  35.7 1.0 reshape.177
  36.7 0.7 gather_fusion
  37.5 0.7 fusion.234
  38.2 1.2 fusion.231
  39.7 0.9 fusion.172
  40.6 32.1 %psum.35 = f32[3,1152]{1,0:T(4,128)S(1)} all-reduce(f32[3,1152]{1,0:T(4,128)S(1)} %fusion.172), channel_id=1, replica_groups=mesh['gy_0'=8,'gy_1'=4,'gy_2'=2,'gz_0'=2,'gz_1'=4] {'gy_0'}, use_global_device_ids=true, to_apply=%region_1.2 | all-reduce | flops 3456 | bytes 27648 | tf_op jit(solution)/shard_map/psum | solution.py:21
  72.7 19.3 %psum.36 = f32[3,1152]{1,0:T(4,128)S(1)} all-reduce(f32[3,1152]{1,0:T(4,128)S(1)} %psum.35), channel_id=1, replica_groups=mesh['gy_0'=8,'gy_1'=4,'gy_2'=2,'gz_0'=2,'gz_1'=4] {'gy_1'}, use_global_device_ids=true, to_apply=%region_2.3 | all-reduce | flops 3456 | bytes 27648 | tf_op jit(solution)/shard_map/psum | solution.py:21
  91.9 3.4 %psum.37 = f32[3,1152]{1,0:T(4,128)S(1)} all-reduce(f32[3,1152]{1,0:T(4,128)S(1)} %psum.36), channel_id=1, replica_groups=mesh['gy_0'=8,'gy_1'=4,'gy_2'=2,'gz_0'=2,'gz_1'=4] {'gy_2'}, use_global_device_ids=true, to_apply=%region_3.4 | all-reduce | flops 3456 | bytes 27648 | tf_op jit(solution)/shard_map/psum | solution.py:21
  95.3 10.7 %psum.38 = f32[3,1152]{1,0:T(4,128)S(1)} all-reduce(f32[3,1152]{1,0:T(4,128)S(1)} %psum.37), channel_id=1, replica_groups=mesh['gy_0'=8,'gy_1'=4,'gy_2'=2,'gz_0'=2,'gz_1'=4] {'gz_0'}, use_global_device_ids=true, to_apply=%region_4.5 | all-reduce | flops 3456 | bytes 27648 | tf_op jit(solution)/shard_map/psum | solution.py:21
  106.1 22.9 %psum.39 = f32[3,1152]{1,0:T(4,128)S(1)} all-reduce(f32[3,1152]{1,0:T(4,128)S(1)} %psum.38), channel_id=1, replica_groups=mesh['gy_0'=8,'gy_1'=4,'gy_2'=2,'gz_0'=2,'gz_1'=4] {'gz_1'}, use_global_device_ids=true, to_apply=%region_5.6 | all-reduce | flops 3456 | bytes 27648 | tf_op jit(solution)/shard_map/psum | solution.py:21
  130.0 1.2 multiply_bitcast_fusion.2
  131.3 1.2 fusion.96
  132.8 2.6 %fusion.85 = (f32[16,64,128]{2,1,0:T(8,128)}, f32[16,64,128]{2,1,0:T(8,128)}, f32[16,64,128]{2,1,0:T(8,128)}, f32[16,64,128]{2,1,0:T(8,128)}) fusion(f32[16,64,128]{2,1,0:T(8,128)S(1)} %get-tuple-element.18), kind=kLoop, calls=%fused_computation.191 | loop fusion | flops 9437184 | bytes 2621440 | tf_op jit(solution)/shard_map/jit(_where)/select_n | solution.py:62
  135.4 1.1 copy.16
  136.4 1.6 gather_fusion.4
  138.2 1.9 collective-permute-start.7
  140.1 0.8 pad.29
  140.9 1.9 collective-permute-start.2
  142.9 3.3 %collective-permute-start.5 = (f32[3,2,64,128]{3,2,1,0:T(8,128)}, f32[3,2,64,128]{3,2,1,0:T(8,128)S(1)}, u32[]{:S(2)}, u32[]{:S(2)}) collective-permute-start(f32[3,2,64,128]{3,2,1,0:T(8,128)} %get-tuple-element.34), channel_id=1, source_target_pairs={{8,0},{16,8},{24,16},{32,24},{40,32},{48,40},{56,48},{64,56},{72,6... | collective-permute-start | bytes 589832 | tf_op jit(solution)/shard_map/ppermute | solution.py:34
  146.3 1.0 constant_dynamic-update-slice_fusion.4
  147.3 1.0 constant_dynamic-update-slice_fusion.8
  148.2 1.2 constant_dynamic-update-slice_fusion.3
  149.9 1.0 copy-done.5
  151.0 3.7 %select_maximum_fusion = f32[3,20,68,132]{3,2,1,0:T(8,128)} fusion(f32[3,20,2,128]{3,2,1,0:T(2,128)S(1)} %pad.34, f32[3,20,64,128]{3,2,1,0:T(8,128)S(1)} %get-tuple-element.57, f32[3,20,2,128]{3,2,1,0:T(2,128)S(1)} %pad.33), kind=kLoop, calls=%fused_computation.15 | loop fusion | flops 4308480 | bytes 4243200 | tf_op jit(solution)/shard_map/concatenate | solution.py:40
  154.8 19.1 %fusion.27 = f32[3,16,64,128]{3,2,1,0:T(8,128)} fusion(f32[3,16,64,128]{3,2,1,0:T(8,128)S(1)} %copy-done.1, f32[3,20,64,128]{3,2,1,0:T(8,128)} %copy-done.3, f32[3,20,2,128]{3,2,1,0:T(2,128)S(1)} %pad.34, f32[3,20,2,128]{3,2,1,0:T(2,128)S(1)} %pad.33, f32[3,20,64,128]{3,2,1,0:T(8,128)} %copy-done.2, f32[3,20,2,128]{3,2,1,0:T(2,128)S(1)} %pad.30, ...), kind=kOutput, calls=%fused_computation.66 | convolution fusion | flops 64931328 | bytes 29863944 | tf_op jit(solution)/shard_map/dot_general | solution.py:210
  173.9 6.4 %fusion.45 = f32[3,16,64,128]{3,2,1,0:T(8,128)S(1)} fusion(f32[3,16,64,128]{3,2,1,0:T(8,128)} %fusion.27, f32[16,64,128]{2,1,0:T(8,128)} %get-tuple-element.49, f32[16,64,128]{2,1,0:T(8,128)} %get-tuple-element.48, f32[16,64,128]{2,1,0:T(8,128)} %get-tuple-element.17, f32[16,64,128]{2,1,0:T(8,128)} %get-tuple-element.47, f32[16,64,128]{2,1,0:T(8,128)} %get-tuple-element.46), kind=kLoop, calls=%fused_computation.84 | loop fusion | flops 3538944 | bytes 5767168 | tf_op jit(solution)/shard_map/add | solution.py:103
  180.3 4.8 %collective-permute-start.8 = (f32[3,2,64,128]{3,2,1,0:T(8,128)S(1)}, f32[3,2,64,128]{3,2,1,0:T(8,128)S(1)}, u32[]{:S(2)}, u32[]{:S(2)}) collective-permute-start(f32[3,2,64,128]{3,2,1,0:T(8,128)S(1)} %get-tuple-element.15), channel_id=1, source_target_pairs={{8,0},{16,8},{24,16},{32,24},{40,32},{48,40},{56,48},{64,56},{72,6... | collective-permute-start | bytes 589832 | tf_op jit(solution)/shard_map/ppermute | solution.py:53
  185.1 1.9 collective-permute-start.9
  187.1 1.5 fusion.80
  188.8 1.2 collective-permute-done.8
  189.9 4.9 %collective-permute-done.9 = f32[3,2,64,128]{3,2,1,0:T(8,128)S(1)} collective-permute-done((f32[3,2,64,128]{3,2,1,0:T(8,128)S(1)}, f32[3,2,64,128]{3,2,1,0:T(8,128)S(1)}, u32[]{:S(2)}, u32[]{:S(2)}) %collective-permute-start.9) | collective-permute-done | bytes 196640 | tf_op jit(solution)/shard_map/ppermute | solution.py:52
  194.8 1.3 fusion.12
  196.2 3.4 %collective-permute-start.10 = (f32[3,16,2,128]{3,2,1,0:T(2,128)S(1)}, f32[3,16,2,128]{3,2,1,0:T(2,128)S(1)}, u32[]{:S(2)}, u32[]{:S(2)}) collective-permute-start(f32[3,16,2,128]{3,2,1,0:T(2,128)S(1)} %get-tuple-element.13), channel_id=1, source_target_pairs={{1,0},{2,1},{3,2},{4,3},{5,4},{6,5},{7,6},{9,8},{10,9},{11,10},{12... | collective-permute-start | bytes 147464 | tf_op jit(solution)/shard_map/ppermute | solution.py:53
  199.6 2.4 %collective-permute-start.11 = (f32[3,16,2,128]{3,2,1,0:T(2,128)S(1)}, f32[3,16,2,128]{3,2,1,0:T(2,128)S(1)}, u32[]{:S(2)}, u32[]{:S(2)}) collective-permute-start(f32[3,16,2,128]{3,2,1,0:T(2,128)S(1)} %get-tuple-element.14), channel_id=1, source_target_pairs={{0,1},{1,2},{2,3},{3,4},{4,5},{5,6},{6,7},{8,9},{9,10},{10,11},{11... | collective-permute-start | bytes 147464 | tf_op jit(solution)/shard_map/ppermute | solution.py:52
  202.0 1.7 fusion.75
  203.7 7.9 %collective-permute-done.11 = f32[3,16,2,128]{3,2,1,0:T(2,128)S(1)} collective-permute-done((f32[3,16,2,128]{3,2,1,0:T(2,128)S(1)}, f32[3,16,2,128]{3,2,1,0:T(2,128)S(1)}, u32[]{:S(2)}, u32[]{:S(2)}) %collective-permute-start.11) | collective-permute-done | bytes 49184 | tf_op jit(solution)/shard_map/ppermute | solution.py:52
  211.6 2.1 fusion.4
  (86 shorter events, 5.2 us)
Async XLA Ops:
  0.6 8.4 %copy-start = (f32[3,16,64,128]{3,2,1,0:T(8,128)S(1)}, f32[3,16,64,128]{3,2,1,0:T(8,128)}, u32[]{:S(2)}) copy-start(f32[3,16,64,128]{3,2,1,0:T(8,128)} %param.9) | copy-start | bytes 4718596
  0.6 24.6 %copy-start.15 = (s32[1152]{0:T(1024)S(1)}, s32[1152]{0:T(1024)}, u32[]{:S(2)}) copy-start(s32[1152]{0:T(1024)} %param.10) | copy-start | bytes 13828
  0.7 30.8 %copy-start.10 = (f32[3,1152]{1,0:T(4,128)S(1)}, f32[3,1152]{1,0:T(4,128)}, u32[]{:S(2)}) copy-start(f32[3,1152]{1,0:T(4,128)} %param.12) | copy-start | bytes 41476
  0.7 31.8 %copy-start.11 = (s32[3,1152]{1,0:T(4,128)S(1)}, s32[3,1152]{1,0:T(4,128)}, u32[]{:S(2)}) copy-start(s32[3,1152]{1,0:T(4,128)} %param.11) | copy-start | bytes 41476
  2.6 143.7 %collective-permute-start.1 = (f32[3,2,64,128]{3,2,1,0:T(8,128)}, f32[3,2,64,128]{3,2,1,0:T(8,128)}, u32[]{:S(2)}, u32[]{:S(2)}) collective-permute-start(f32[3,2,64,128]{3,2,1,0:T(8,128)} %get-tuple-element.31), channel_id=1, source_target_pairs={{0,8},{8,16},{16,24},{24,32},{32,40},{40,48},{48,56},{56,64},{64,7... | collective-permute-start | bytes 589832 | tf_op jit(solution)/shard_map/ppermute | solution.py:33
  6.3 140.9 %collective-permute-start.4 = (f32[3,2,64,128]{3,2,1,0:T(8,128)}, f32[3,2,64,128]{3,2,1,0:T(8,128)}, u32[]{:S(2)}, u32[]{:S(2)}) collective-permute-start(f32[3,2,64,128]{3,2,1,0:T(8,128)} %get-tuple-element.35), channel_id=1, source_target_pairs={{0,8},{8,16},{16,24},{24,32},{32,40},{40,48},{48,56},{56,64},{64,7... | collective-permute-start | bytes 589832 | tf_op jit(solution)/shard_map/ppermute | solution.py:33
  9.7 128.4 %collective-permute-start = (f32[3,16,2,128]{3,2,1,0:T(2,128)}, f32[3,16,2,128]{3,2,1,0:T(2,128)}, u32[]{:S(2)}, u32[]{:S(2)}) collective-permute-start(f32[3,16,2,128]{3,2,1,0:T(2,128)} %get-tuple-element.28), channel_id=1, source_target_pairs={{0,1},{1,2},{2,3},{3,4},{4,5},{5,6},{6,7},{8,9},{9,10},{10,11},{11... | collective-permute-start | bytes 147464 | tf_op jit(solution)/shard_map/ppermute | solution.py:33
  13.1 127.8 %collective-permute-start.3 = (f32[3,16,2,128]{3,2,1,0:T(2,128)}, f32[3,16,2,128]{3,2,1,0:T(2,128)S(1)}, u32[]{:S(2)}, u32[]{:S(2)}) collective-permute-start(f32[3,16,2,128]{3,2,1,0:T(2,128)} %get-tuple-element.29), channel_id=1, source_target_pairs={{1,0},{2,1},{3,2},{4,3},{5,4},{6,5},{7,6},{9,8},{10,9},{11,10},{12... | collective-permute-start | bytes 147464 | tf_op jit(solution)/shard_map/ppermute | solution.py:34
  23.3 119.6 %collective-permute-start.6 = (f32[3,16,2,128]{3,2,1,0:T(2,128)}, f32[3,16,2,128]{3,2,1,0:T(2,128)S(1)}, u32[]{:S(2)}, u32[]{:S(2)}) collective-permute-start(f32[3,16,2,128]{3,2,1,0:T(2,128)} %get-tuple-element.32), channel_id=1, source_target_pairs={{0,1},{1,2},{2,3},{3,4},{4,5},{5,6},{6,7},{8,9},{9,10},{10,11},{11... | collective-permute-start | bytes 147464 | tf_op jit(solution)/shard_map/ppermute | solution.py:33
  33.5 39.2 %copy-start.16 = (s32[9]{0:T(128)}, s32[9]{0:T(128)S(1)}, u32[]{:S(2)}) copy-start(s32[9]{0:T(128)S(1)} %get-tuple-element.7) | copy-start | bytes 112
  33.5 96.1 %copy-start.12 = (f32[1152]{0:T(1024)S(1)}, f32[1152]{0:T(1024)}, u32[]{:S(2)}) copy-start(f32[1152]{0:T(1024)} %param.14) | copy-start | bytes 13828
  33.5 96.1 %copy-start.13 = (f32[1152]{0:T(1024)S(1)}, f32[1152]{0:T(1024)}, u32[]{:S(2)}) copy-start(f32[1152]{0:T(1024)} %param.13) | copy-start | bytes 13828
  33.6 96.5 %copy-start.1 = (f32[3,16,64,128]{3,2,1,0:T(8,128)S(1)}, f32[3,16,64,128]{3,2,1,0:T(8,128)}, u32[]{:S(2)}) copy-start(f32[3,16,64,128]{3,2,1,0:T(8,128)} %param.8) | copy-start | bytes 4718596
  132.7 5.4 %copy-start.7 = (f32[3,16,2,128]{3,2,1,0:T(2,128)S(1)}, f32[3,16,2,128]{3,2,1,0:T(2,128)}, u32[]{:S(2)}) copy-start(f32[3,16,2,128]{3,2,1,0:T(2,128)} %get-tuple-element.33) | copy-start | bytes 147460
  135.4 14.1 %copy-start.6 = (f32[3,1152]{1,0:T(4,128)}, f32[3,1152]{1,0:T(4,128)S(1)}, u32[]{:S(2)}) copy-start(f32[3,1152]{1,0:T(4,128)S(1)} %pad_maximum_fusion.9) | copy-start | bytes 41476
  138.2 8.1 %collective-permute-start.7 = (f32[3,16,2,128]{3,2,1,0:T(2,128)S(1)}, f32[3,16,2,128]{3,2,1,0:T(2,128)S(1)}, u32[]{:S(2)}, u32[]{:S(2)}) collective-permute-start(f32[3,16,2,128]{3,2,1,0:T(2,128)S(1)} %copy-done.7), channel_id=1, source_target_pairs={{1,0},{2,1},{3,2},{4,3},{5,4},{6,5},{7,6},{9,8},{10,9},{11,10},{12... | collective-permute-start | bytes 147464 | tf_op jit(solution)/shard_map/ppermute | solution.py:34
  140.9 8.5 %collective-permute-start.2 = (f32[3,2,64,128]{3,2,1,0:T(8,128)}, f32[3,2,64,128]{3,2,1,0:T(8,128)S(1)}, u32[]{:S(2)}, u32[]{:S(2)}) collective-permute-start(f32[3,2,64,128]{3,2,1,0:T(8,128)} %get-tuple-element.30), channel_id=1, source_target_pairs={{8,0},{16,8},{24,16},{32,24},{40,32},{48,40},{56,48},{64,56},{72,6... | collective-permute-start | bytes 589832 | tf_op jit(solution)/shard_map/ppermute | solution.py:34
  142.9 8.0 %collective-permute-start.5 = (f32[3,2,64,128]{3,2,1,0:T(8,128)}, f32[3,2,64,128]{3,2,1,0:T(8,128)S(1)}, u32[]{:S(2)}, u32[]{:S(2)}) collective-permute-start(f32[3,2,64,128]{3,2,1,0:T(8,128)} %get-tuple-element.34), channel_id=1, source_target_pairs={{8,0},{16,8},{24,16},{32,24},{40,32},{48,40},{56,48},{64,56},{72,6... | collective-permute-start | bytes 589832 | tf_op jit(solution)/shard_map/ppermute | solution.py:34
  149.4 5.3 %copy-start.8 = (f32[3,18,64,128]{3,2,1,0:T(8,128)}, f32[3,18,64,128]{3,2,1,0:T(8,128)S(1)}, u32[]{:S(2)}) copy-start(f32[3,18,64,128]{3,2,1,0:T(8,128)S(1)} %get-tuple-element.22) | copy-start | bytes 5308420
  149.5 5.3 %copy-start.9 = (f32[3,18,64,128]{3,2,1,0:T(8,128)}, f32[3,18,64,128]{3,2,1,0:T(8,128)S(1)}, u32[]{:S(2)}) copy-start(f32[3,18,64,128]{3,2,1,0:T(8,128)S(1)} %get-tuple-element.71) | copy-start | bytes 5308420
  149.5 1.4 copy-start.5
  149.5 5.2 %copy-start.2 = (f32[3,20,64,128]{3,2,1,0:T(8,128)}, f32[3,20,64,128]{3,2,1,0:T(8,128)S(1)}, u32[]{:S(2)}) copy-start(f32[3,20,64,128]{3,2,1,0:T(8,128)S(1)} %get-tuple-element.53) | copy-start | bytes 5898244
  151.0 3.8 %copy-start.4 = (f32[3,18,64,128]{3,2,1,0:T(8,128)}, f32[3,18,64,128]{3,2,1,0:T(8,128)S(1)}, u32[]{:S(2)}) copy-start(f32[3,18,64,128]{3,2,1,0:T(8,128)S(1)} %get-tuple-element.56) | copy-start | bytes 5308420
  151.0 3.8 %copy-start.3 = (f32[3,20,64,128]{3,2,1,0:T(8,128)}, f32[3,20,64,128]{3,2,1,0:T(8,128)S(1)}, u32[]{:S(2)}) copy-start(f32[3,20,64,128]{3,2,1,0:T(8,128)S(1)} %get-tuple-element.57) | copy-start | bytes 5898244
  151.0 3.8 %copy-start.14 = (f32[9,64]{1,0:T(8,128)S(1)}, f32[9,64]{1,0:T(8,128)}, u32[]{:S(2)}) copy-start(f32[9,64]{1,0:T(8,128)} %get-tuple-element.68) | copy-start | bytes 6916
  151.0 3.8 %copy-start.17 = (s32[9]{0:T(128)S(1)}, s32[9]{0:T(128)}, u32[]{:S(2)}) copy-start(s32[9]{0:T(128)} %copy-done.16) | copy-start | bytes 112
  180.3 9.6 %collective-permute-start.8 = (f32[3,2,64,128]{3,2,1,0:T(8,128)S(1)}, f32[3,2,64,128]{3,2,1,0:T(8,128)S(1)}, u32[]{:S(2)}, u32[]{:S(2)}) collective-permute-start(f32[3,2,64,128]{3,2,1,0:T(8,128)S(1)} %get-tuple-element.15), channel_id=1, source_target_pairs={{8,0},{16,8},{24,16},{32,24},{40,32},{48,40},{56,48},{64,56},{72,6... | collective-permute-start | bytes 589832 | tf_op jit(solution)/shard_map/ppermute | solution.py:53
  185.1 9.7 %collective-permute-start.9 = (f32[3,2,64,128]{3,2,1,0:T(8,128)S(1)}, f32[3,2,64,128]{3,2,1,0:T(8,128)S(1)}, u32[]{:S(2)}, u32[]{:S(2)}) collective-permute-start(f32[3,2,64,128]{3,2,1,0:T(8,128)S(1)} %get-tuple-element.16), channel_id=1, source_target_pairs={{0,8},{8,16},{16,24},{24,32},{32,40},{40,48},{48,56},{56,64},{64,7... | collective-permute-start | bytes 589832 | tf_op jit(solution)/shard_map/ppermute | solution.py:52
  196.2 7.5 %collective-permute-start.10 = (f32[3,16,2,128]{3,2,1,0:T(2,128)S(1)}, f32[3,16,2,128]{3,2,1,0:T(2,128)S(1)}, u32[]{:S(2)}, u32[]{:S(2)}) collective-permute-start(f32[3,16,2,128]{3,2,1,0:T(2,128)S(1)} %get-tuple-element.13), channel_id=1, source_target_pairs={{1,0},{2,1},{3,2},{4,3},{5,4},{6,5},{7,6},{9,8},{10,9},{11,10},{12... | collective-permute-start | bytes 147464 | tf_op jit(solution)/shard_map/ppermute | solution.py:53
  199.6 12.0 %collective-permute-start.11 = (f32[3,16,2,128]{3,2,1,0:T(2,128)S(1)}, f32[3,16,2,128]{3,2,1,0:T(2,128)S(1)}, u32[]{:S(2)}, u32[]{:S(2)}) collective-permute-start(f32[3,16,2,128]{3,2,1,0:T(2,128)S(1)} %get-tuple-element.14), channel_id=1, source_target_pairs={{0,1},{1,2},{2,3},{3,4},{4,5},{5,6},{6,7},{8,9},{9,10},{10,11},{11... | collective-permute-start | bytes 147464 | tf_op jit(solution)/shard_map/ppermute | solution.py:52
where the time goes:
time: 214 us
  blocking collectives  88.4 us (41%)
  starting transfers between devices  38 us (18%)
  other arithmetic  29.1 us (14%)
  matrix products  23.5 us (11%)
  local copies, waits for them, and re-layouts  18.8 us (9%)
  waiting for transfers between devices  13.9 us (6%)
    psum x5, blocking collectives, by_axis(): x = lax.psum(x, axis)  88.4 us
    dot_general x1, matrix products, on_device(): jnp.dot(spread.reshape(-1, spread.shape[3]), table_x.T, precision=highest...  19.1 us
    ppermute x4, starting transfers between devices, with_halo(): lax.ppermute(initial, axis, [(b, a) for a, b in up])  15.6 us
    ppermute x2, waiting for transfers between devices, with_halo_2(): before = lax.ppermute(last, axis, up)  12.7 us
    ppermute x4, starting transfers between devices, with_halo(): lax.ppermute(last, axis, up)  9.88 us
    add x3, other arithmetic, remesh_padded(): total = total + remesh_kernel(offset - moved)[None] * part  9.84 us
    ppermute x2, starting transfers between devices, with_halo_2(): after = lax.ppermute(initial, axis, down)  8.16 us
    select_n x5, other arithmetic, remesh_kernel(): return jnp.where(mag < 1.0, inner, jnp.where(mag < 2.0, outer, 0.0))  6.53 us
  transfers between devices with their start and end apart: 12, of which 3 were waited for; matrix products, arithmetic and copies ran while one was open for 17% of the time, Pallas kernels for 0%

commit v1 on v0

--- a/solution.py
+++ b/solution.py
@@ -18,7 +18,8 @@
 
 def by_axis(x, axes):
     for axis in axes:
-        x = lax.psum(x, axis)
+        parts = lax.all_gather(x, axis, axis=0, tiled=False)
+        x = parts.sum(axis=0)
     return x
 
 

time: 214 us -> 201 us (0.939)
  blocking collectives: 88.4 us -> 65.3 us
  starting transfers between devices: 38 us -> 49 us
    psum x5 -> x0, blocking collectives: 88.4 us -> none  [by_axis(): x = lax.psum(x, axis)]
    all_gather x0 -> x5, blocking collectives: none -> 65.3 us  [by_axis(): parts = lax.all_gather(x, axis, axis=0, tiled=False)]
    ppermute x4, starting transfers between devices: 15.6 us -> 26.6 us  [with_halo(): lax.ppermute(initial, axis, [(b, a) for a, b in up])]
  transfers between devices with their start and end apart: 12 -> 12, of which waited for: 3 -> 3; matrix products, arithmetic and copies ran while one was open for 17% -> 18% of each run, Pallas kernels for 0% -> 0%
where the time goes in v1:
time: 201 us; the launch traced here: 200 us
  blocking collectives  65.3 us (32%)
  starting transfers between devices  49 us (24%)
  other arithmetic  29.2 us (15%)
  matrix products  23.5 us (12%)
  local copies, waits for them, and re-layouts  19 us (9%)
  waiting for transfers between devices  12.5 us (6%)
    all_gather x5, blocking collectives, by_axis(): parts = lax.all_gather(x, axis, axis=0, tiled=False)  65.3 us
    ppermute x4, starting transfers between devices, with_halo(): lax.ppermute(initial, axis, [(b, a) for a, b in up])  26.6 us
    dot_general x1, matrix products, on_device(): jnp.dot(spread.reshape(-1, spread.shape[3]), table_x.T, precision=highest...  19.1 us
    ppermute x2, waiting for transfers between devices, with_halo_2(): before = lax.ppermute(last, axis, up)  12 us
    ppermute x4, starting transfers between devices, with_halo(): lax.ppermute(last, axis, up)  9.88 us
    add x3, other arithmetic, remesh_padded(): total = total + remesh_kernel(offset - moved)[None] * part  9.84 us
    ppermute x2, starting transfers between devices, with_halo_2(): after = lax.ppermute(initial, axis, down)  6.69 us
    select_n x5, other arithmetic, remesh_kernel(): return jnp.where(mag < 1.0, inner, jnp.where(mag < 2.0, outer, 0.0))  6.52 us
  transfers between devices with their start and end apart: 12, of which 3 were waited for; matrix products, arithmetic and copies ran while one was open for 18% of the time, Pallas kernels for 0%

profile of v1, /device:TPU:96, one launch (start us, length us, event | category | flops | bytes accessed | tf_op | source)
XLA Modules:
  0.0 200.3 jit_solution(15446815508385143966)
XLA Ops:
  0.7 1.9 fusion.255
  2.6 1.9 collective-permute-start.1
  4.5 1.8 fusion.257
  6.3 2.7 %collective-permute-start.4 = (f32[3,2,64,128]{3,2,1,0:T(8,128)}, f32[3,2,64,128]{3,2,1,0:T(8,128)}, u32[]{:S(2)}, u32[]{:S(2)}) collective-permute-start(f32[3,2,64,128]{3,2,1,0:T(8,128)} %get-tuple-element.39), channel_id=1, source_target_pairs={{0,8},{8,16},{16,24},{24,32},{32,40},{40,48},{48,56},{56,64},{64,7... | collective-permute-start | bytes 589832 | tf_op jit(solution)/shard_map/ppermute | solution.py:34
  9.0 0.7 fusion.254
  9.7 3.4 %collective-permute-start = (f32[3,16,2,128]{3,2,1,0:T(2,128)}, f32[3,16,2,128]{3,2,1,0:T(2,128)}, u32[]{:S(2)}, u32[]{:S(2)}) collective-permute-start(f32[3,16,2,128]{3,2,1,0:T(2,128)} %get-tuple-element.32), channel_id=1, source_target_pairs={{0,1},{1,2},{2,3},{3,4},{4,5},{5,6},{6,7},{8,9},{9,10},{10,11},{11... | collective-permute-start | bytes 147464 | tf_op jit(solution)/shard_map/ppermute | solution.py:34
  13.1 8.5 %collective-permute-start.3 = (f32[3,16,2,128]{3,2,1,0:T(2,128)}, f32[3,16,2,128]{3,2,1,0:T(2,128)S(1)}, u32[]{:S(2)}, u32[]{:S(2)}) collective-permute-start(f32[3,16,2,128]{3,2,1,0:T(2,128)} %get-tuple-element.33), channel_id=1, source_target_pairs={{1,0},{2,1},{3,2},{4,3},{5,4},{6,5},{7,6},{9,8},{10,9},{11,10},{12... | collective-permute-start | bytes 147464 | tf_op jit(solution)/shard_map/ppermute | solution.py:35
  21.6 1.7 fusion.256
  23.3 1.9 collective-permute-start.6
  25.3 5.0 %sort.17 = (s32[1152]{0:T(1024)}, s32[1152]{0:T(1024)S(1)}) sort(s32[1152]{0:T(1024)S(1)} %get-tuple-element.65, s32[1152]{0:T(1024)S(1)} %iota.43), dimensions={0}, to_apply=%region_0.1 | sort | flops 12672 | bytes 18432 | tf_op jit(solution)/shard_map/jit(argsort)/sort | solution.py:183
  30.8 0.7 gather_fusion.3
  33.5 2.1 %convolution_bitcast_fusion = f32[3072,9]{0,1:T(8,128)} fusion(f32[3072,128]{1,0:T(8,128)S(1)} %bitcast.54, f32[9]{0:T(128)S(1)} %get-tuple-element.14, s32[9]{0:T(128)S(1)} %get-tuple-element.11), kind=kOutput, calls=%fused_computation.18 | convolution fusion | flops 42490368 | bytes 1683528 | tf_op jit(solution)/shard_map/dot_general | solution.py:196
  35.6 1.1 reshape.177
  36.8 0.7 gather_fusion
  37.6 0.7 fusion.233
  38.3 1.2 fusion.230
  39.8 0.9 convolution_bitcast_fusion.1
  40.7 30.1 %all-gather.5 = f32[8,3,1152]{2,1,0:T(4,128)S(1)} all-gather(f32[1,3,1152]{2,1,0:T(4,128)S(1)} %convolution_bitcast_fusion.1), channel_id=2, replica_groups=mesh['gy_0'=8,'gy_1'=4,'gy_2'=2,'gz_0'=2,'gz_1'=4] {'gy_0'}, dimensions={0}, use_global_device_ids=true | all-gather | bytes 124416 | tf_op jit(solution)/shard_map/all_gather | solution.py:21
  70.8 13.2 %all-gather.6 = f32[4,3,1152]{2,1,0:T(4,128)S(1)} all-gather(f32[1,3,1152]{2,1,0:T(4,128)S(1)} %bitcast.61), channel_id=3, replica_groups=mesh['gy_0'=8,'gy_1'=4,'gy_2'=2,'gz_0'=2,'gz_1'=4] {'gy_1'}, dimensions={0}, use_global_device_ids=true | all-gather | bytes 69120 | tf_op jit(solution)/shard_map/all_gather | solution.py:21
  83.9 1.8 all-gather.7
  85.8 8.3 %all-gather.8 = f32[2,3,1152]{2,1,0:T(4,128)S(1)} all-gather(f32[1,3,1152]{2,1,0:T(4,128)S(1)} %bitcast.58), channel_id=5, replica_groups=mesh['gy_0'=8,'gy_1'=4,'gy_2'=2,'gz_0'=2,'gz_1'=4] {'gz_0'}, dimensions={0}, use_global_device_ids=true | all-gather | bytes 41472 | tf_op jit(solution)/shard_map/all_gather | solution.py:21
  94.1 11.9 %all-gather.9 = f32[4,3,1152]{2,1,0:T(4,128)S(1)} all-gather(f32[1,3,1152]{2,1,0:T(4,128)S(1)} %bitcast.60), channel_id=6, replica_groups=mesh['gy_0'=8,'gy_1'=4,'gy_2'=2,'gz_0'=2,'gz_1'=4] {'gz_1'}, dimensions={0}, use_global_device_ids=true | all-gather | bytes 69120 | tf_op jit(solution)/shard_map/all_gather | solution.py:21
  107.2 1.2 multiply_bitcast_fusion.2
  108.4 1.2 fusion.96
  109.9 2.6 %fusion.85 = (f32[16,64,128]{2,1,0:T(8,128)}, f32[16,64,128]{2,1,0:T(8,128)}, f32[16,64,128]{2,1,0:T(8,128)}, f32[16,64,128]{2,1,0:T(8,128)}) fusion(f32[16,64,128]{2,1,0:T(8,128)S(1)} %get-tuple-element.22), kind=kLoop, calls=%fused_computation.192 | loop fusion | flops 9437184 | bytes 2621440 | tf_op jit(solution)/shard_map/jit(_where)/select_n | solution.py:63
  112.5 1.1 copy.23
  113.6 1.6 gather_fusion.4
  115.3 9.9 %collective-permute-start.7 = (f32[3,16,2,128]{3,2,1,0:T(2,128)S(1)}, f32[3,16,2,128]{3,2,1,0:T(2,128)S(1)}, u32[]{:S(2)}, u32[]{:S(2)}) collective-permute-start(f32[3,16,2,128]{3,2,1,0:T(2,128)S(1)} %copy-done.7), channel_id=1, source_target_pairs={{1,0},{2,1},{3,2},{4,3},{5,4},{6,5},{7,6},{9,8},{10,9},{11,10},{12... | collective-permute-start | bytes 147464 | tf_op jit(solution)/shard_map/ppermute | solution.py:35
  125.3 0.8 pad.29
  126.1 1.9 collective-permute-start.2
  128.1 6.3 %collective-permute-start.5 = (f32[3,2,64,128]{3,2,1,0:T(8,128)}, f32[3,2,64,128]{3,2,1,0:T(8,128)S(1)}, u32[]{:S(2)}, u32[]{:S(2)}) collective-permute-start(f32[3,2,64,128]{3,2,1,0:T(8,128)} %get-tuple-element.38), channel_id=1, source_target_pairs={{8,0},{16,8},{24,16},{32,24},{40,32},{48,40},{56,48},{64,56},{72,6... | collective-permute-start | bytes 589832 | tf_op jit(solution)/shard_map/ppermute | solution.py:35
  134.4 1.0 constant_dynamic-update-slice_fusion.4
  135.4 1.0 constant_dynamic-update-slice_fusion.8
  136.3 1.2 constant_dynamic-update-slice_fusion.3
  138.0 1.0 copy-done.5
  139.1 3.7 %select_maximum_fusion = f32[3,20,68,132]{3,2,1,0:T(8,128)} fusion(f32[3,20,2,128]{3,2,1,0:T(2,128)S(1)} %pad.34, f32[3,20,64,128]{3,2,1,0:T(8,128)S(1)} %get-tuple-element.61, f32[3,20,2,128]{3,2,1,0:T(2,128)S(1)} %pad.33), kind=kLoop, calls=%fused_computation.15 | loop fusion | flops 4308480 | bytes 4243200 | tf_op jit(solution)/shard_map/concatenate | solution.py:41
  142.9 19.1 %fusion.27 = f32[3,16,64,128]{3,2,1,0:T(8,128)} fusion(f32[3,16,64,128]{3,2,1,0:T(8,128)S(1)} %copy-done.1, f32[3,20,64,128]{3,2,1,0:T(8,128)} %copy-done.3, f32[3,20,2,128]{3,2,1,0:T(2,128)S(1)} %pad.34, f32[3,20,2,128]{3,2,1,0:T(2,128)S(1)} %pad.33, f32[3,20,64,128]{3,2,1,0:T(8,128)} %copy-done.2, f32[3,20,2,128]{3,2,1,0:T(2,128)S(1)} %pad.30, ...), kind=kOutput, calls=%fused_computation.67 | convolution fusion | flops 64931328 | bytes 29863944 | tf_op jit(solution)/shard_map/dot_general | solution.py:211
  162.0 6.4 %fusion.45 = f32[3,16,64,128]{3,2,1,0:T(8,128)S(1)} fusion(f32[3,16,64,128]{3,2,1,0:T(8,128)} %fusion.27, f32[16,64,128]{2,1,0:T(8,128)} %get-tuple-element.53, f32[16,64,128]{2,1,0:T(8,128)} %get-tuple-element.52, f32[16,64,128]{2,1,0:T(8,128)} %get-tuple-element.21, f32[16,64,128]{2,1,0:T(8,128)} %get-tuple-element.51, f32[16,64,128]{2,1,0:T(8,128)} %get-tuple-element.50), kind=kLoop, calls=%fused_computation.85 | loop fusion | flops 3538944 | bytes 5767168 | tf_op jit(solution)/shard_map/add | solution.py:104
  168.4 4.8 %collective-permute-start.8 = (f32[3,2,64,128]{3,2,1,0:T(8,128)S(1)}, f32[3,2,64,128]{3,2,1,0:T(8,128)S(1)}, u32[]{:S(2)}, u32[]{:S(2)}) collective-permute-start(f32[3,2,64,128]{3,2,1,0:T(8,128)S(1)} %get-tuple-element.19), channel_id=1, source_target_pairs={{8,0},{16,8},{24,16},{32,24},{40,32},{48,40},{56,48},{64,56},{72,6... | collective-permute-start | bytes 589832 | tf_op jit(solution)/shard_map/ppermute | solution.py:54
  173.2 1.9 collective-permute-start.9
  175.2 1.5 fusion.80
  177.4 5.6 %collective-permute-done.9 = f32[3,2,64,128]{3,2,1,0:T(8,128)S(1)} collective-permute-done((f32[3,2,64,128]{3,2,1,0:T(8,128)S(1)}, f32[3,2,64,128]{3,2,1,0:T(8,128)S(1)}, u32[]{:S(2)}, u32[]{:S(2)}) %collective-permute-start.9) | collective-permute-done | bytes 196640 | tf_op jit(solution)/shard_map/ppermute | solution.py:53
  182.9 1.3 fusion.12
  184.3 1.9 collective-permute-start.10
  186.2 3.9 %collective-permute-start.11 = (f32[3,16,2,128]{3,2,1,0:T(2,128)S(1)}, f32[3,16,2,128]{3,2,1,0:T(2,128)S(1)}, u32[]{:S(2)}, u32[]{:S(2)}) collective-permute-start(f32[3,16,2,128]{3,2,1,0:T(2,128)S(1)} %get-tuple-element.18), channel_id=1, source_target_pairs={{0,1},{1,2},{2,3},{3,4},{4,5},{5,6},{6,7},{8,9},{9,10},{10,11},{11... | collective-permute-start | bytes 147464 | tf_op jit(solution)/shard_map/ppermute | solution.py:53
  190.2 1.7 fusion.75
  191.8 6.4 %collective-permute-done.11 = f32[3,16,2,128]{3,2,1,0:T(2,128)S(1)} collective-permute-done((f32[3,16,2,128]{3,2,1,0:T(2,128)S(1)}, f32[3,16,2,128]{3,2,1,0:T(2,128)S(1)}, u32[]{:S(2)}, u32[]{:S(2)}) %collective-permute-start.11) | collective-permute-done | bytes 49184 | tf_op jit(solution)/shard_map/ppermute | solution.py:53
  198.2 2.1 %fusion.4 = f32[3,16,64,128]{3,2,1,0:T(8,128)} fusion(f32[3,16,2,128]{3,2,1,0:T(2,128)S(1)} %collective-permute-done.11, f32[3,16,64,128]{3,2,1,0:T(8,128)S(1)} %fusion.12, f32[3,16,2,128]{3,2,1,0:T(2,128)S(1)} %collective-permute-done.10, f32[16,64,128]{2,1,0:T(8,128)S(1)} %get-tuple-element.46, f32[16,64,128]{2,1,0:T(8,128)S(1)} %get-tuple-element.47, ...), kind=kLoop, calls=%fused_computation.44 | loop fusion | flops 5111808 | bytes 5865472 | tf_op jit(solution)/shard_map/add | solution.py:104
  (91 shorter events, 5.2 us)
Async XLA Ops:
  0.6 8.4 %copy-start = (f32[3,16,64,128]{3,2,1,0:T(8,128)S(1)}, f32[3,16,64,128]{3,2,1,0:T(8,128)}, u32[]{:S(2)}) copy-start(f32[3,16,64,128]{3,2,1,0:T(8,128)} %param.9) | copy-start | bytes 4718596
  0.6 24.6 %copy-start.15 = (s32[1152]{0:T(1024)S(1)}, s32[1152]{0:T(1024)}, u32[]{:S(2)}) copy-start(s32[1152]{0:T(1024)} %param.10) | copy-start | bytes 13828
  0.7 30.8 %copy-start.10 = (s32[3,1152]{1,0:T(4,128)S(1)}, s32[3,1152]{1,0:T(4,128)}, u32[]{:S(2)}) copy-start(s32[3,1152]{1,0:T(4,128)} %param.11) | copy-start | bytes 41476
  0.7 31.8 %copy-start.11 = (f32[3,1152]{1,0:T(4,128)S(1)}, f32[3,1152]{1,0:T(4,128)}, u32[]{:S(2)}) copy-start(f32[3,1152]{1,0:T(4,128)} %param.12) | copy-start | bytes 41476
  2.6 131.8 %collective-permute-start.1 = (f32[3,2,64,128]{3,2,1,0:T(8,128)}, f32[3,2,64,128]{3,2,1,0:T(8,128)}, u32[]{:S(2)}, u32[]{:S(2)}) collective-permute-start(f32[3,2,64,128]{3,2,1,0:T(8,128)} %get-tuple-element.35), channel_id=1, source_target_pairs={{0,8},{8,16},{16,24},{24,32},{32,40},{40,48},{48,56},{56,64},{64,7... | collective-permute-start | bytes 589832 | tf_op jit(solution)/shard_map/ppermute | solution.py:34
  6.3 129.0 %collective-permute-start.4 = (f32[3,2,64,128]{3,2,1,0:T(8,128)}, f32[3,2,64,128]{3,2,1,0:T(8,128)}, u32[]{:S(2)}, u32[]{:S(2)}) collective-permute-start(f32[3,2,64,128]{3,2,1,0:T(8,128)} %get-tuple-element.39), channel_id=1, source_target_pairs={{0,8},{8,16},{16,24},{24,32},{32,40},{40,48},{48,56},{56,64},{64,7... | collective-permute-start | bytes 589832 | tf_op jit(solution)/shard_map/ppermute | solution.py:34
  9.7 105.6 %collective-permute-start = (f32[3,16,2,128]{3,2,1,0:T(2,128)}, f32[3,16,2,128]{3,2,1,0:T(2,128)}, u32[]{:S(2)}, u32[]{:S(2)}) collective-permute-start(f32[3,16,2,128]{3,2,1,0:T(2,128)} %get-tuple-element.32), channel_id=1, source_target_pairs={{0,1},{1,2},{2,3},{3,4},{4,5},{5,6},{6,7},{8,9},{9,10},{10,11},{11... | collective-permute-start | bytes 147464 | tf_op jit(solution)/shard_map/ppermute | solution.py:34
  13.1 113.0 %collective-permute-start.3 = (f32[3,16,2,128]{3,2,1,0:T(2,128)}, f32[3,16,2,128]{3,2,1,0:T(2,128)S(1)}, u32[]{:S(2)}, u32[]{:S(2)}) collective-permute-start(f32[3,16,2,128]{3,2,1,0:T(2,128)} %get-tuple-element.33), channel_id=1, source_target_pairs={{1,0},{2,1},{3,2},{4,3},{5,4},{6,5},{7,6},{9,8},{10,9},{11,10},{12... | collective-permute-start | bytes 147464 | tf_op jit(solution)/shard_map/ppermute | solution.py:35
  23.3 104.8 %collective-permute-start.6 = (f32[3,16,2,128]{3,2,1,0:T(2,128)}, f32[3,16,2,128]{3,2,1,0:T(2,128)S(1)}, u32[]{:S(2)}, u32[]{:S(2)}) collective-permute-start(f32[3,16,2,128]{3,2,1,0:T(2,128)} %get-tuple-element.36), channel_id=1, source_target_pairs={{0,1},{1,2},{2,3},{3,4},{4,5},{5,6},{6,7},{8,9},{9,10},{10,11},{11... | collective-permute-start | bytes 147464 | tf_op jit(solution)/shard_map/ppermute | solution.py:34
  33.5 4.0 %copy-start.16 = (f32[9]{0:T(128)}, f32[9]{0:T(128)S(1)}, u32[]{:S(2)}) copy-start(f32[9]{0:T(128)S(1)} %get-tuple-element.14) | copy-start | bytes 112
  35.6 71.1 %copy-start.12 = (f32[1152]{0:T(1024)S(1)}, f32[1152]{0:T(1024)}, u32[]{:S(2)}) copy-start(f32[1152]{0:T(1024)} %param.14) | copy-start | bytes 13828
  35.6 71.1 %copy-start.13 = (f32[1152]{0:T(1024)S(1)}, f32[1152]{0:T(1024)}, u32[]{:S(2)}) copy-start(f32[1152]{0:T(1024)} %param.13) | copy-start | bytes 13828
  35.6 71.5 %copy-start.1 = (f32[3,16,64,128]{3,2,1,0:T(8,128)S(1)}, f32[3,16,64,128]{3,2,1,0:T(8,128)}, u32[]{:S(2)}) copy-start(f32[3,16,64,128]{3,2,1,0:T(8,128)} %param.8) | copy-start | bytes 4718596
  109.9 5.4 %copy-start.7 = (f32[3,16,2,128]{3,2,1,0:T(2,128)S(1)}, f32[3,16,2,128]{3,2,1,0:T(2,128)}, u32[]{:S(2)}) copy-start(f32[3,16,2,128]{3,2,1,0:T(2,128)} %get-tuple-element.37) | copy-start | bytes 147460
  112.5 25.0 %copy-start.6 = (f32[3,1152]{1,0:T(4,128)}, f32[3,1152]{1,0:T(4,128)S(1)}, u32[]{:S(2)}) copy-start(f32[3,1152]{1,0:T(4,128)S(1)} %pad_maximum_fusion.9) | copy-start | bytes 41476
  115.3 19.0 %collective-permute-start.7 = (f32[3,16,2,128]{3,2,1,0:T(2,128)S(1)}, f32[3,16,2,128]{3,2,1,0:T(2,128)S(1)}, u32[]{:S(2)}, u32[]{:S(2)}) collective-permute-start(f32[3,16,2,128]{3,2,1,0:T(2,128)S(1)} %copy-done.7), channel_id=1, source_target_pairs={{1,0},{2,1},{3,2},{4,3},{5,4},{6,5},{7,6},{9,8},{10,9},{11,10},{12... | collective-permute-start | bytes 147464 | tf_op jit(solution)/shard_map/ppermute | solution.py:35
  126.1 11.5 %collective-permute-start.2 = (f32[3,2,64,128]{3,2,1,0:T(8,128)}, f32[3,2,64,128]{3,2,1,0:T(8,128)S(1)}, u32[]{:S(2)}, u32[]{:S(2)}) collective-permute-start(f32[3,2,64,128]{3,2,1,0:T(8,128)} %get-tuple-element.34), channel_id=1, source_target_pairs={{8,0},{16,8},{24,16},{32,24},{40,32},{48,40},{56,48},{64,56},{72,6... | collective-permute-start | bytes 589832 | tf_op jit(solution)/shard_map/ppermute | solution.py:35
  128.1 11.0 %collective-permute-start.5 = (f32[3,2,64,128]{3,2,1,0:T(8,128)}, f32[3,2,64,128]{3,2,1,0:T(8,128)S(1)}, u32[]{:S(2)}, u32[]{:S(2)}) collective-permute-start(f32[3,2,64,128]{3,2,1,0:T(8,128)} %get-tuple-element.38), channel_id=1, source_target_pairs={{8,0},{16,8},{24,16},{32,24},{40,32},{48,40},{56,48},{64,56},{72,6... | collective-permute-start | bytes 589832 | tf_op jit(solution)/shard_map/ppermute | solution.py:35
  137.5 5.3 %copy-start.8 = (f32[3,18,64,128]{3,2,1,0:T(8,128)}, f32[3,18,64,128]{3,2,1,0:T(8,128)S(1)}, u32[]{:S(2)}) copy-start(f32[3,18,64,128]{3,2,1,0:T(8,128)S(1)} %get-tuple-element.26) | copy-start | bytes 5308420
  137.6 5.3 %copy-start.9 = (f32[3,18,64,128]{3,2,1,0:T(8,128)}, f32[3,18,64,128]{3,2,1,0:T(8,128)S(1)}, u32[]{:S(2)}) copy-start(f32[3,18,64,128]{3,2,1,0:T(8,128)S(1)} %get-tuple-element.75) | copy-start | bytes 5308420
  137.6 1.4 copy-start.5
  137.6 5.2 %copy-start.2 = (f32[3,20,64,128]{3,2,1,0:T(8,128)}, f32[3,20,64,128]{3,2,1,0:T(8,128)S(1)}, u32[]{:S(2)}) copy-start(f32[3,20,64,128]{3,2,1,0:T(8,128)S(1)} %get-tuple-element.57) | copy-start | bytes 5898244
  139.1 3.8 %copy-start.4 = (f32[3,18,64,128]{3,2,1,0:T(8,128)}, f32[3,18,64,128]{3,2,1,0:T(8,128)S(1)}, u32[]{:S(2)}) copy-start(f32[3,18,64,128]{3,2,1,0:T(8,128)S(1)} %get-tuple-element.60) | copy-start | bytes 5308420
  139.1 3.8 %copy-start.3 = (f32[3,20,64,128]{3,2,1,0:T(8,128)}, f32[3,20,64,128]{3,2,1,0:T(8,128)S(1)}, u32[]{:S(2)}) copy-start(f32[3,20,64,128]{3,2,1,0:T(8,128)S(1)} %get-tuple-element.61) | copy-start | bytes 5898244
  139.1 3.8 %copy-start.14 = (f32[9,64]{1,0:T(8,128)S(1)}, f32[9,64]{1,0:T(8,128)}, u32[]{:S(2)}) copy-start(f32[9,64]{1,0:T(8,128)} %get-tuple-element.72) | copy-start | bytes 6916
  139.1 3.8 %copy-start.17 = (f32[9]{0:T(128)S(1)}, f32[9]{0:T(128)}, u32[]{:S(2)}) copy-start(f32[9]{0:T(128)} %copy-done.16) | copy-start | bytes 112
  168.4 8.9 %collective-permute-start.8 = (f32[3,2,64,128]{3,2,1,0:T(8,128)S(1)}, f32[3,2,64,128]{3,2,1,0:T(8,128)S(1)}, u32[]{:S(2)}, u32[]{:S(2)}) collective-permute-start(f32[3,2,64,128]{3,2,1,0:T(8,128)S(1)} %get-tuple-element.19), channel_id=1, source_target_pairs={{8,0},{16,8},{24,16},{32,24},{40,32},{48,40},{56,48},{64,56},{72,6... | collective-permute-start | bytes 589832 | tf_op jit(solution)/shard_map/ppermute | solution.py:54
  173.2 9.7 %collective-permute-start.9 = (f32[3,2,64,128]{3,2,1,0:T(8,128)S(1)}, f32[3,2,64,128]{3,2,1,0:T(8,128)S(1)}, u32[]{:S(2)}, u32[]{:S(2)}) collective-permute-start(f32[3,2,64,128]{3,2,1,0:T(8,128)S(1)} %get-tuple-element.20), channel_id=1, source_target_pairs={{0,8},{8,16},{16,24},{24,32},{32,40},{40,48},{48,56},{56,64},{64,7... | collective-permute-start | bytes 589832 | tf_op jit(solution)/shard_map/ppermute | solution.py:53
  184.3 7.5 %collective-permute-start.10 = (f32[3,16,2,128]{3,2,1,0:T(2,128)S(1)}, f32[3,16,2,128]{3,2,1,0:T(2,128)S(1)}, u32[]{:S(2)}, u32[]{:S(2)}) collective-permute-start(f32[3,16,2,128]{3,2,1,0:T(2,128)S(1)} %get-tuple-element.17), channel_id=1, source_target_pairs={{1,0},{2,1},{3,2},{4,3},{5,4},{6,5},{7,6},{9,8},{10,9},{11,10},{12... | collective-permute-start | bytes 147464 | tf_op jit(solution)/shard_map/ppermute | solution.py:54
  186.2 12.0 %collective-permute-start.11 = (f32[3,16,2,128]{3,2,1,0:T(2,128)S(1)}, f32[3,16,2,128]{3,2,1,0:T(2,128)S(1)}, u32[]{:S(2)}, u32[]{:S(2)}) collective-permute-start(f32[3,16,2,128]{3,2,1,0:T(2,128)S(1)} %get-tuple-element.18), channel_id=1, source_target_pairs={{0,1},{1,2},{2,3},{3,4},{4,5},{5,6},{6,7},{8,9},{9,10},{10,11},{11... | collective-permute-start | bytes 147464 | tf_op jit(solution)/shard_map/ppermute | solution.py:53
